TPU v7x, 32 devices: a whole 2x2x4 slice. The times are simulated.
32 devices in a mesh: node: 16 (over z, y, x), hand: 2 (over core).
Axes of the slice: x: 2, y: 2, z: 4, core: 2. Of those that a mesh axis runs over, the one named last changes fastest.
Arguments:
- ranges: bfloat16 [512, 128, 1326], P('node', None, 'hand'), may hold values from 0.00019931793 to 0.0039978027
- strengths: int32 [512, 1326], P('node'), may hold values from 0 to 399
- live_hands: int32 [512, 1326], P('node'), may hold values 0 or 1
- pot_sizes: float32 [512, 128], P('node'), may hold values from 1 to 16
- action_counts: int32 [512], P('node'), may hold values from 1 to 8
- parents: int32 [512], P('node'), may hold values from 0 to 63
- turn_counts: int32 [16], replicated, may hold values from 1 to 4
- root_reach: float32 [16, 2, 1326], P(None, None, 'hand'), may hold values from 0.01 to 1
Outputs:
- turn_values: float32 [16, 2, 1326], P('node', None, 'hand')
- exploitability: float32 [], replicated
All inputs are finite; a program needn't handle non-finite values. No bound on the sum of `live_hands` on one device may be relied on, other than what follows from the above.
Results may differ from a plain program's by a relative error of at most 0.0003.
Values may be sent and summed in bfloat16 or wider, within the bound.
A program may use at most 128 MiB of HBM per device.

v0:
```python
import jax
import jax.numpy as jnp
import numpy as np
from jax import lax
from jax.sharding import PartitionSpec as P

ACT = 8
GROUPS = 8
TACT = 4


def card_pairs(wanted):
    first_list = []
    second_list = []
    for lower_card in range(52):
        for upper_card in range(lower_card + 1, 52):
            first_list.append(lower_card)
            second_list.append(upper_card)
    return (
        jnp.asarray(np.array(first_list[:wanted], dtype=np.int32)),
        jnp.asarray(np.array(second_list[:wanted], dtype=np.int32)),
    )


def pair_compat(row_first, row_second, col_first, col_second):
    shared = (row_first[:, None] == col_first[None, :]) | (
        row_first[:, None] == col_second[None, :]
    )
    shared = (
        shared
        | (row_second[:, None] == col_first[None, :])
        | (row_second[:, None] == col_second[None, :])
    )
    return jnp.where(shared, 0.0, 1.0).astype(jnp.float32)


def showdown_block(compat, packed):
    left_strength, left_live, right_strength, right_live, reach_block = packed
    signs = jnp.sign((left_strength[:, :, None] - right_strength[:, None, :]).astype(jnp.float32))
    matrix = (signs * compat[None] * left_live[:, :, None] * right_live[:, None, :]).astype(
        jnp.bfloat16
    )
    return jnp.einsum("nij,nlj->nli", matrix, reach_block, preferred_element_type=jnp.float32)


def river_from(raw_values, pots, legal):
    count = raw_values.shape[0]
    width = raw_values.shape[2]
    values = (raw_values * pots[:, :, None]).reshape(count, 2, GROUPS, ACT, width)
    usable = jnp.arange(ACT)[None, :] < legal[:, None]
    return jnp.where(usable[:, None, None, :, None], values, -1e30).max(axis=3).sum(axis=2)


def turn_best(sums, legal):
    hand_half = sums.shape[1] // 2
    shaped = sums.reshape(-1, TACT, 2, hand_half)
    usable = jnp.arange(TACT)[None, :] < legal[:, None]
    return jnp.where(usable[:, :, None, None], shaped, -1e30).max(axis=1)


def local(
    ranges, strengths, live_hands, pot_sizes, action_counts, parents, turn_counts, root_reach
):
    node_count, line_cols, hand_half = ranges.shape
    hands_all = strengths.shape[1]
    hand_start = lax.axis_index("hand") * hand_half
    first_card, second_card = card_pairs(hands_all)
    live_all = live_hands.astype(jnp.float32)
    blocks = node_count // 4

    def grouped(array):
        return array.reshape((blocks, 4) + array.shape[1:])

    row_first = lax.dynamic_slice_in_dim(first_card, hand_start, hand_half, 0)
    row_second = lax.dynamic_slice_in_dim(second_card, hand_start, hand_half, 0)
    row_strength = lax.dynamic_slice_in_dim(strengths, hand_start, hand_half, 1)
    row_live = lax.dynamic_slice_in_dim(live_all, hand_start, hand_half, 1)
    compat = pair_compat(row_first, row_second, first_card, second_card)

    def one_block(packed):
        return showdown_block(compat, packed)

    added = lax.map(
        one_block,
        (
            grouped(row_strength),
            grouped(row_live),
            grouped(strengths),
            grouped(live_all),
            grouped(lax.all_gather(ranges, "hand", axis=2, tiled=True)),
        ),
    )
    raw_values = added.reshape(jnp.zeros((node_count, line_cols, hand_half), jnp.float32).shape)
    river_best = river_from(raw_values, pot_sizes, action_counts)
    flat_best = river_best.reshape(node_count, 2 * hand_half)
    turns_all = turn_counts.shape[0]
    turns_mine = turns_all // lax.axis_size("node")
    turn_start = lax.axis_index("node") * turns_mine
    parents_all = turns_all * TACT
    onehot = (parents[None, :] == jnp.arange(parents_all, dtype=jnp.int32)[:, None]).astype(
        jnp.float32
    )
    local_sums = jnp.dot(onehot, flat_best, precision=lax.Precision.HIGHEST)
    totals = lax.psum(local_sums, "node")
    values_all = turn_best(totals, turn_counts)
    exploitability = lax.psum(jnp.sum(root_reach * values_all), "hand")
    turn_values = lax.dynamic_slice_in_dim(values_all, turn_start, turns_mine, 0)
    return (turn_values, exploitability)


def solution(mesh):
    in_specs = (
        P("node", None, "hand"),
        P("node", None),
        P("node", None),
        P("node", None),
        P("node"),
        P("node"),
        P(),
        P(None, None, "hand"),
    )
    out_specs = (P("node", None, "hand"), P())
    return jax.shard_map(local, mesh=mesh, in_specs=in_specs, out_specs=out_specs, check_vma=False)
```

profile of v0, /device:TPU:0, one launch (start us, length us, event | category | flops | bytes accessed | tf_op | source)
XLA Modules:
  0.0 278.7 jit_solution(3800787151186367840)
XLA Ops:
  14.4 20.9 %all-gather.2.cloned.1.call-done = bf16[32,128,1326]{1,0,2:T(8,128)(2,1)} async-done(((bf16[32,128,663]{1,0,2:T(8,128)(2,1)}), bf16[32,128,1326]{1,0,2:T(8,128)(2,1)}) %all-gather.2.cloned.1.call-update) | async-done | bytes 10862608 | tf_op jit(solution)/shard_map/all_gather | solution.py:90
  35.3 89.9 %while.11 = (s32[]{:T(128)}, f32[8,4,128,663]{2,3,1,0:T(8,128)}, bf16[8,4,128,1326]{2,1,0,3:T(4,128)(2,1)}, s32[8,4,663]{2,1,0:T(4,128)S(1)}, s32[8,4,1326]{2,1,...) while((s32[]{:T(128)}, f32[8,4,128,663]{2,3,1,0:T(8,128)}, ...), condition=%wide.region_1.2_spmd.clone, body=%wide.region_0.1_spmd.clone.sunk | while | flops 931886272 | bytes 12673953 | solution.py:83
  35.3 1.6 constant_dynamic-slice_fusion.5
  37.0 2.2 or_select_fusion.2
  39.2 7.4 %fusion.9 = f32[8,4,128,663]{2,3,1,0:T(8,128)} fusion(f32[8,4,128,663]{2,3,1,0:T(8,128)} %get-tuple-element.197, s32[]{:T(128)} %get-tuple-element.196, f32[4,1326]{1,0:T(4,128)S(1)} %dynamic-slice_bitcast_fusion.8, f32[4,663]{1,0:T(4,128)S(1)} %dynamic-slice_bitcast_fusion.9, f32[663,1326]{1,0:T(8,128)S(1)} %or_select_fusion.2, ...), kind=kOutput, calls=%fused_computation.5.clone.1 | convolution fusion | flops 924853184 | bytes 6298408 | tf_op jit(solution)/shard_map/while/body/eval_jaxpr/nij,nlj->nli/dot_general | solution.py:43
  46.6 1.6 constant_dynamic-slice_fusion.5
  48.3 2.2 or_select_fusion.2
  50.5 7.3 %fusion.9 = f32[8,4,128,663]{2,3,1,0:T(8,128)} fusion(f32[8,4,128,663]{2,3,1,0:T(8,128)} %get-tuple-element.197, s32[]{:T(128)} %get-tuple-element.196, f32[4,1326]{1,0:T(4,128)S(1)} %dynamic-slice_bitcast_fusion.8, f32[4,663]{1,0:T(4,128)S(1)} %dynamic-slice_bitcast_fusion.9, f32[663,1326]{1,0:T(8,128)S(1)} %or_select_fusion.2, ...), kind=kOutput, calls=%fused_computation.5.clone.1 | convolution fusion | flops 924853184 | bytes 6298408 | tf_op jit(solution)/shard_map/while/body/eval_jaxpr/nij,nlj->nli/dot_general | solution.py:43
  59.5 2.2 or_select_fusion.2
  61.7 7.3 %fusion.9 = f32[8,4,128,663]{2,3,1,0:T(8,128)} fusion(f32[8,4,128,663]{2,3,1,0:T(8,128)} %get-tuple-element.197, s32[]{:T(128)} %get-tuple-element.196, f32[4,1326]{1,0:T(4,128)S(1)} %dynamic-slice_bitcast_fusion.8, f32[4,663]{1,0:T(4,128)S(1)} %dynamic-slice_bitcast_fusion.9, f32[663,1326]{1,0:T(8,128)S(1)} %or_select_fusion.2, ...), kind=kOutput, calls=%fused_computation.5.clone.1 | convolution fusion | flops 924853184 | bytes 6298408 | tf_op jit(solution)/shard_map/while/body/eval_jaxpr/nij,nlj->nli/dot_general | solution.py:43
  70.7 2.2 or_select_fusion.2
  73.0 7.3 %fusion.9 = f32[8,4,128,663]{2,3,1,0:T(8,128)} fusion(f32[8,4,128,663]{2,3,1,0:T(8,128)} %get-tuple-element.197, s32[]{:T(128)} %get-tuple-element.196, f32[4,1326]{1,0:T(4,128)S(1)} %dynamic-slice_bitcast_fusion.8, f32[4,663]{1,0:T(4,128)S(1)} %dynamic-slice_bitcast_fusion.9, f32[663,1326]{1,0:T(8,128)S(1)} %or_select_fusion.2, ...), kind=kOutput, calls=%fused_computation.5.clone.1 | convolution fusion | flops 924853184 | bytes 6298408 | tf_op jit(solution)/shard_map/while/body/eval_jaxpr/nij,nlj->nli/dot_general | solution.py:43
  81.9 2.2 or_select_fusion.2
  84.2 7.3 %fusion.9 = f32[8,4,128,663]{2,3,1,0:T(8,128)} fusion(f32[8,4,128,663]{2,3,1,0:T(8,128)} %get-tuple-element.197, s32[]{:T(128)} %get-tuple-element.196, f32[4,1326]{1,0:T(4,128)S(1)} %dynamic-slice_bitcast_fusion.8, f32[4,663]{1,0:T(4,128)S(1)} %dynamic-slice_bitcast_fusion.9, f32[663,1326]{1,0:T(8,128)S(1)} %or_select_fusion.2, ...), kind=kOutput, calls=%fused_computation.5.clone.1 | convolution fusion | flops 924853184 | bytes 6298408 | tf_op jit(solution)/shard_map/while/body/eval_jaxpr/nij,nlj->nli/dot_general | solution.py:43
  93.2 2.2 or_select_fusion.2
  95.4 7.3 %fusion.9 = f32[8,4,128,663]{2,3,1,0:T(8,128)} fusion(f32[8,4,128,663]{2,3,1,0:T(8,128)} %get-tuple-element.197, s32[]{:T(128)} %get-tuple-element.196, f32[4,1326]{1,0:T(4,128)S(1)} %dynamic-slice_bitcast_fusion.8, f32[4,663]{1,0:T(4,128)S(1)} %dynamic-slice_bitcast_fusion.9, f32[663,1326]{1,0:T(8,128)S(1)} %or_select_fusion.2, ...), kind=kOutput, calls=%fused_computation.5.clone.1 | convolution fusion | flops 924853184 | bytes 6298408 | tf_op jit(solution)/shard_map/while/body/eval_jaxpr/nij,nlj->nli/dot_general | solution.py:43
  104.4 2.2 or_select_fusion.2
  106.7 7.3 %fusion.9 = f32[8,4,128,663]{2,3,1,0:T(8,128)} fusion(f32[8,4,128,663]{2,3,1,0:T(8,128)} %get-tuple-element.197, s32[]{:T(128)} %get-tuple-element.196, f32[4,1326]{1,0:T(4,128)S(1)} %dynamic-slice_bitcast_fusion.8, f32[4,663]{1,0:T(4,128)S(1)} %dynamic-slice_bitcast_fusion.9, f32[663,1326]{1,0:T(8,128)S(1)} %or_select_fusion.2, ...), kind=kOutput, calls=%fused_computation.5.clone.1 | convolution fusion | flops 924853184 | bytes 6298408 | tf_op jit(solution)/shard_map/while/body/eval_jaxpr/nij,nlj->nli/dot_general | solution.py:43
  115.6 2.2 or_select_fusion.2
  117.9 7.3 %fusion.9 = f32[8,4,128,663]{2,3,1,0:T(8,128)} fusion(f32[8,4,128,663]{2,3,1,0:T(8,128)} %get-tuple-element.197, s32[]{:T(128)} %get-tuple-element.196, f32[4,1326]{1,0:T(4,128)S(1)} %dynamic-slice_bitcast_fusion.8, f32[4,663]{1,0:T(4,128)S(1)} %dynamic-slice_bitcast_fusion.9, f32[663,1326]{1,0:T(8,128)S(1)} %or_select_fusion.2, ...), kind=kOutput, calls=%fused_computation.5.clone.1 | convolution fusion | flops 924853184 | bytes 6298408 | tf_op jit(solution)/shard_map/while/body/eval_jaxpr/nij,nlj->nli/dot_general | solution.py:43
  125.2 12.0 %copy.22 = f32[8,4,128,663]{3,2,1,0:T(8,128)} copy(f32[8,4,128,663]{2,3,1,0:T(8,128)} %get-tuple-element.44) | data formatting | bytes 21725184 | tf_op jit(solution)/shard_map/while | solution.py:83
  137.1 16.8 %select_reduce_fusion = f32[32,2,8,663]{3,2,1,0:T(8,128)S(1)} fusion(f32[32,2,8,8,663]{4,3,2,1,0:T(8,128)} %bitcast.31, f32[32,2,8,8]{3,2,1,0:T(8,128)S(1)} %copy.24, pred[32,8]{1,0:T(8,128)(4,1)S(1)} %iota_compare_fusion.2), kind=kLoop, calls=%fused_computation.12 | loop fusion | flops 7807488 | bytes 12237056 | tf_op jit(solution)/shard_map/reduce_max | solution.py:51
  156.2 109.9 %all-reduce.2.cloned.1.call-done = f32[16,4,2,663]{3,2,1,0:T(2,128)} async-done(((f32[16,4,2,663]{3,2,1,0:T(2,128)}), f32[16,4,2,663]{3,2,1,0:T(2,128)}) %all-reduce.2.cloned.1.call-update) | async-done | bytes 339472 | tf_op jit(solution)/shard_map/psum | solution.py:104
  268.8 3.1 %psum.15 = f32[]{:T(128)} all-reduce(f32[]{:T(128)} %multiply_reduce_fusion), channel_id=1, replica_groups=mesh['node'=16,'hand'=2] {'hand'}, use_global_device_ids=true, to_apply=%region_7.8 | all-reduce | flops 1 | bytes 8 | tf_op jit(solution)/shard_map/psum | solution.py:106
  (69 shorter events, 22.0 us)
Async XLA Ops:
  7.2 28.1 %all-gather.2.cloned.1.call-start = ((), (), s32[]{:S(2)}) async-start(), calls=%async_computation | async-start | bytes 16293888 | tf_op jit(solution)/shard_map/all_gather | solution.py:90
  7.9 258.2 %all-reduce.2.cloned.1.call-start = ((), (), s32[]{:S(2)}) async-start(), calls=%async_computation.1 | async-start | bytes 786432 | tf_op jit(solution)/shard_map/psum | solution.py:104
  137.1 17.5 %copy-start.1 = (s32[32]{0:T(128)S(1)}, s32[32]{0:T(128)}, u32[]{:S(2)}) copy-start(s32[32]{0:T(128)} %param.17) | copy-start | bytes 388
  137.1 18.9 %copy-start.2 = (s32[16]{0:T(128)S(1)}, s32[16]{0:T(128)}, u32[]{:S(2)}) copy-start(s32[16]{0:T(128)} %param.18) | copy-start | bytes 196
  137.1 130.4 %copy-start = (f32[16,2,663]{2,1,0:T(2,128)S(1)}, f32[16,2,663]{2,1,0:T(2,128)}, u32[]{:S(2)}) copy-start(f32[16,2,663]{2,1,0:T(2,128)} %param.19) | copy-start | bytes 254596
Sparse Core Ops, SparseCore 0:
  9.5 25.7 all-gather.1
  156.2 109.8 all-reduce.1
where the time goes:
time: 280 us; the launch traced here: 279 us
  waiting for transfers between devices  132 us (47%)
  matrix products  58.7 us (21%)
  other arithmetic  39.1 us (14%)
  local copies, waits for them, and re-layouts  31.7 us (11%)
  between operations  14.2 us (5%)
  blocking collectives  3.08 us (1%)
    psum x1, waiting for transfers between devices, local(): totals = lax.psum(local_sums, 'node')  110 us
    dot_general x8, matrix products, showdown_block(): jnp.einsum('nij,nlj->nli', matrix, reach_block, preferred_element_type=jn...  58.4 us
    all_gather x1, waiting for transfers between devices, local(): lax.all_gather(ranges, 'hand', axis=2, tiled=True)  20.9 us
    select_n x8, other arithmetic, pair_compat(): return jnp.where(shared, 0.0, 1.0).astype(jnp.float32)  17.9 us
    reduce_max x1, other arithmetic, river_from(): jnp.where(usable[:, None, None, :, None], values, -1e+30).max(axis=3)  16.8 us
    dynamic_slice x8, local copies, waits for them, and re-layouts, local(): lax.map(one_block, (grouped(row_strength), grouped(row_live), grouped(str...  12.8 us
    while x1, local copies, waits for them, and re-layouts, local(): lax.map(one_block, (grouped(row_strength), grouped(row_live), grouped(str...  12 us
  transfers between devices with their start and end apart: 2, of which 2 were waited for; matrix products, arithmetic and copies ran while one was open for 2% of the time, Pallas kernels for 0%

commit v1 on v0

--- a/solution.py
+++ b/solution.py
@@ -101,7 +101,9 @@
         jnp.float32
     )
     local_sums = jnp.dot(onehot, flat_best, precision=lax.Precision.HIGHEST)
-    totals = lax.psum(local_sums, "node")
+    totals = local_sums
+    for hop in (1, 2, 4, 8):
+        totals = totals + lax.ppermute(totals, "node", [(dev, dev ^ hop) for dev in range(16)])
     values_all = turn_best(totals, turn_counts)
     exploitability = lax.psum(jnp.sum(root_reach * values_all), "hand")
     turn_values = lax.dynamic_slice_in_dim(values_all, turn_start, turns_mine, 0)

time: 280 us -> 215 us (0.77)
  waiting for transfers between devices: 132 us -> 59.6 us
  starting transfers between devices: 0.08 us -> 8.19 us
    psum x1 -> x0, waiting for transfers between devices: 110 us -> none  [local(): totals = lax.psum(local_sums, 'node')]
    ppermute x0 -> x4, waiting for transfers between devices: none -> 38 us  [local(): lax.ppermute(totals, 'node', [(dev, dev ^ hop) for dev in range(16)])]
    ppermute x0 -> x4, starting transfers between devices: none -> 8.16 us  [local(): lax.ppermute(totals, 'node', [(dev, dev ^ hop) for dev in range(16)])]
  transfers between devices with their start and end apart: 2 -> 5, of which waited for: 2 -> 5; matrix products, arithmetic and copies ran while one was open for 2% -> 3% of each run, Pallas kernels for 0% -> 0%
where the time goes in v1:
time: 215 us; the launch traced here: 213 us
  waiting for transfers between devices  59.6 us (28%)
  matrix products  58.7 us (27%)
  other arithmetic  38.2 us (18%)
  local copies, waits for them, and re-layouts  31 us (14%)
  between operations  14.2 us (7%)
  starting transfers between devices  8.19 us (4%)
  blocking collectives  3.08 us (1%)
    dot_general x8, matrix products, showdown_block(): jnp.einsum('nij,nlj->nli', matrix, reach_block, preferred_element_type=jn...  58.4 us
    ppermute x4, waiting for transfers between devices, local(): lax.ppermute(totals, 'node', [(dev, dev ^ hop) for dev in range(16)])  38 us
    all_gather x1, waiting for transfers between devices, local(): lax.all_gather(ranges, 'hand', axis=2, tiled=True)  21 us
    select_n x8, other arithmetic, pair_compat(): return jnp.where(shared, 0.0, 1.0).astype(jnp.float32)  17.9 us
    reduce_max x1, other arithmetic, river_from(): jnp.where(usable[:, None, None, :, None], values, -1e+30).max(axis=3)  16.8 us
    dynamic_slice x8, local copies, waits for them, and re-layouts, local(): lax.map(one_block, (grouped(row_strength), grouped(row_live), grouped(str...  12.8 us
    while x1, local copies, waits for them, and re-layouts, local(): lax.map(one_block, (grouped(row_strength), grouped(row_live), grouped(str...  12 us
    ppermute x4, starting transfers between devices, local(): lax.ppermute(totals, 'node', [(dev, dev ^ hop) for dev in range(16)])  8.16 us
  transfers between devices with their start and end apart: 5, of which 5 were waited for; matrix products, arithmetic and copies ran while one was open for 3% of the time, Pallas kernels for 0%

profile of v1, /device:TPU:0, one launch (start us, length us, event | category | flops | bytes accessed | tf_op | source)
XLA Modules:
  0.0 213.3 jit_solution(7463860705130200226)
XLA Ops:
  14.3 21.0 %all-gather.2.cloned.1.call-done = bf16[32,128,1326]{1,0,2:T(8,128)(2,1)} async-done(((bf16[32,128,663]{1,0,2:T(8,128)(2,1)}), bf16[32,128,1326]{1,0,2:T(8,128)(2,1)}) %all-gather.2.cloned.1.call-update) | async-done | bytes 10862608 | tf_op jit(solution)/shard_map/all_gather | solution.py:90
  35.3 89.9 %while.11 = (s32[]{:T(128)}, f32[8,4,128,663]{2,3,1,0:T(8,128)}, bf16[8,4,128,1326]{2,1,0,3:T(4,128)(2,1)}, s32[8,4,663]{2,1,0:T(4,128)S(1)}, s32[8,4,1326]{2,1,...) while((s32[]{:T(128)}, f32[8,4,128,663]{2,3,1,0:T(8,128)}, ...), condition=%wide.region_1.2_spmd.clone, body=%wide.region_0.1_spmd.clone.sunk | while | flops 931886272 | bytes 12673953 | solution.py:83
  37.0 2.2 %or_select_fusion.2 = f32[663,1326]{1,0:T(8,128)S(1)} fusion(s32[1326]{0:T(1024)} %get-tuple-element.217, s32[1326]{0:T(1024)} %get-tuple-element.216, s32[663]{0:T(1024)S(1)} %get-tuple-element.218, s32[663]{0:T(1024)S(1)} %get-tuple-element.215), kind=kLoop, calls=%fused_computation.3.clone.1 | loop fusion | flops 7033104 | bytes 3532464 | tf_op jit(solution)/shard_map/jit(_where)/select_n | solution.py:34
  39.2 7.3 %fusion.9 = f32[8,4,128,663]{2,3,1,0:T(8,128)} fusion(f32[8,4,128,663]{2,3,1,0:T(8,128)} %get-tuple-element.197, s32[]{:T(128)} %get-tuple-element.196, f32[4,1326]{1,0:T(4,128)S(1)} %dynamic-slice_bitcast_fusion.8, f32[4,663]{1,0:T(4,128)S(1)} %dynamic-slice_bitcast_fusion.9, f32[663,1326]{1,0:T(8,128)S(1)} %or_select_fusion.2, ...), kind=kOutput, calls=%fused_computation.5.clone.1 | convolution fusion | flops 924853184 | bytes 6298408 | tf_op jit(solution)/shard_map/while/body/eval_jaxpr/nij,nlj->nli/dot_general | solution.py:43
  48.3 2.2 %or_select_fusion.2 = f32[663,1326]{1,0:T(8,128)S(1)} fusion(s32[1326]{0:T(1024)} %get-tuple-element.217, s32[1326]{0:T(1024)} %get-tuple-element.216, s32[663]{0:T(1024)S(1)} %get-tuple-element.218, s32[663]{0:T(1024)S(1)} %get-tuple-element.215), kind=kLoop, calls=%fused_computation.3.clone.1 | loop fusion | flops 7033104 | bytes 3532464 | tf_op jit(solution)/shard_map/jit(_where)/select_n | solution.py:34
  50.5 7.3 %fusion.9 = f32[8,4,128,663]{2,3,1,0:T(8,128)} fusion(f32[8,4,128,663]{2,3,1,0:T(8,128)} %get-tuple-element.197, s32[]{:T(128)} %get-tuple-element.196, f32[4,1326]{1,0:T(4,128)S(1)} %dynamic-slice_bitcast_fusion.8, f32[4,663]{1,0:T(4,128)S(1)} %dynamic-slice_bitcast_fusion.9, f32[663,1326]{1,0:T(8,128)S(1)} %or_select_fusion.2, ...), kind=kOutput, calls=%fused_computation.5.clone.1 | convolution fusion | flops 924853184 | bytes 6298408 | tf_op jit(solution)/shard_map/while/body/eval_jaxpr/nij,nlj->nli/dot_general | solution.py:43
  59.5 2.2 %or_select_fusion.2 = f32[663,1326]{1,0:T(8,128)S(1)} fusion(s32[1326]{0:T(1024)} %get-tuple-element.217, s32[1326]{0:T(1024)} %get-tuple-element.216, s32[663]{0:T(1024)S(1)} %get-tuple-element.218, s32[663]{0:T(1024)S(1)} %get-tuple-element.215), kind=kLoop, calls=%fused_computation.3.clone.1 | loop fusion | flops 7033104 | bytes 3532464 | tf_op jit(solution)/shard_map/jit(_where)/select_n | solution.py:34
  61.7 7.3 %fusion.9 = f32[8,4,128,663]{2,3,1,0:T(8,128)} fusion(f32[8,4,128,663]{2,3,1,0:T(8,128)} %get-tuple-element.197, s32[]{:T(128)} %get-tuple-element.196, f32[4,1326]{1,0:T(4,128)S(1)} %dynamic-slice_bitcast_fusion.8, f32[4,663]{1,0:T(4,128)S(1)} %dynamic-slice_bitcast_fusion.9, f32[663,1326]{1,0:T(8,128)S(1)} %or_select_fusion.2, ...), kind=kOutput, calls=%fused_computation.5.clone.1 | convolution fusion | flops 924853184 | bytes 6298408 | tf_op jit(solution)/shard_map/while/body/eval_jaxpr/nij,nlj->nli/dot_general | solution.py:43
  70.7 2.2 %or_select_fusion.2 = f32[663,1326]{1,0:T(8,128)S(1)} fusion(s32[1326]{0:T(1024)} %get-tuple-element.217, s32[1326]{0:T(1024)} %get-tuple-element.216, s32[663]{0:T(1024)S(1)} %get-tuple-element.218, s32[663]{0:T(1024)S(1)} %get-tuple-element.215), kind=kLoop, calls=%fused_computation.3.clone.1 | loop fusion | flops 7033104 | bytes 3532464 | tf_op jit(solution)/shard_map/jit(_where)/select_n | solution.py:34
  73.0 7.3 %fusion.9 = f32[8,4,128,663]{2,3,1,0:T(8,128)} fusion(f32[8,4,128,663]{2,3,1,0:T(8,128)} %get-tuple-element.197, s32[]{:T(128)} %get-tuple-element.196, f32[4,1326]{1,0:T(4,128)S(1)} %dynamic-slice_bitcast_fusion.8, f32[4,663]{1,0:T(4,128)S(1)} %dynamic-slice_bitcast_fusion.9, f32[663,1326]{1,0:T(8,128)S(1)} %or_select_fusion.2, ...), kind=kOutput, calls=%fused_computation.5.clone.1 | convolution fusion | flops 924853184 | bytes 6298408 | tf_op jit(solution)/shard_map/while/body/eval_jaxpr/nij,nlj->nli/dot_general | solution.py:43
  81.9 2.2 %or_select_fusion.2 = f32[663,1326]{1,0:T(8,128)S(1)} fusion(s32[1326]{0:T(1024)} %get-tuple-element.217, s32[1326]{0:T(1024)} %get-tuple-element.216, s32[663]{0:T(1024)S(1)} %get-tuple-element.218, s32[663]{0:T(1024)S(1)} %get-tuple-element.215), kind=kLoop, calls=%fused_computation.3.clone.1 | loop fusion | flops 7033104 | bytes 3532464 | tf_op jit(solution)/shard_map/jit(_where)/select_n | solution.py:34
  84.2 7.3 %fusion.9 = f32[8,4,128,663]{2,3,1,0:T(8,128)} fusion(f32[8,4,128,663]{2,3,1,0:T(8,128)} %get-tuple-element.197, s32[]{:T(128)} %get-tuple-element.196, f32[4,1326]{1,0:T(4,128)S(1)} %dynamic-slice_bitcast_fusion.8, f32[4,663]{1,0:T(4,128)S(1)} %dynamic-slice_bitcast_fusion.9, f32[663,1326]{1,0:T(8,128)S(1)} %or_select_fusion.2, ...), kind=kOutput, calls=%fused_computation.5.clone.1 | convolution fusion | flops 924853184 | bytes 6298408 | tf_op jit(solution)/shard_map/while/body/eval_jaxpr/nij,nlj->nli/dot_general | solution.py:43
  93.2 2.2 %or_select_fusion.2 = f32[663,1326]{1,0:T(8,128)S(1)} fusion(s32[1326]{0:T(1024)} %get-tuple-element.217, s32[1326]{0:T(1024)} %get-tuple-element.216, s32[663]{0:T(1024)S(1)} %get-tuple-element.218, s32[663]{0:T(1024)S(1)} %get-tuple-element.215), kind=kLoop, calls=%fused_computation.3.clone.1 | loop fusion | flops 7033104 | bytes 3532464 | tf_op jit(solution)/shard_map/jit(_where)/select_n | solution.py:34
  95.4 7.3 %fusion.9 = f32[8,4,128,663]{2,3,1,0:T(8,128)} fusion(f32[8,4,128,663]{2,3,1,0:T(8,128)} %get-tuple-element.197, s32[]{:T(128)} %get-tuple-element.196, f32[4,1326]{1,0:T(4,128)S(1)} %dynamic-slice_bitcast_fusion.8, f32[4,663]{1,0:T(4,128)S(1)} %dynamic-slice_bitcast_fusion.9, f32[663,1326]{1,0:T(8,128)S(1)} %or_select_fusion.2, ...), kind=kOutput, calls=%fused_computation.5.clone.1 | convolution fusion | flops 924853184 | bytes 6298408 | tf_op jit(solution)/shard_map/while/body/eval_jaxpr/nij,nlj->nli/dot_general | solution.py:43
  106.6 7.3 %fusion.9 = f32[8,4,128,663]{2,3,1,0:T(8,128)} fusion(f32[8,4,128,663]{2,3,1,0:T(8,128)} %get-tuple-element.197, s32[]{:T(128)} %get-tuple-element.196, f32[4,1326]{1,0:T(4,128)S(1)} %dynamic-slice_bitcast_fusion.8, f32[4,663]{1,0:T(4,128)S(1)} %dynamic-slice_bitcast_fusion.9, f32[663,1326]{1,0:T(8,128)S(1)} %or_select_fusion.2, ...), kind=kOutput, calls=%fused_computation.5.clone.1 | convolution fusion | flops 924853184 | bytes 6298408 | tf_op jit(solution)/shard_map/while/body/eval_jaxpr/nij,nlj->nli/dot_general | solution.py:43
  117.8 7.3 %fusion.9 = f32[8,4,128,663]{2,3,1,0:T(8,128)} fusion(f32[8,4,128,663]{2,3,1,0:T(8,128)} %get-tuple-element.197, s32[]{:T(128)} %get-tuple-element.196, f32[4,1326]{1,0:T(4,128)S(1)} %dynamic-slice_bitcast_fusion.8, f32[4,663]{1,0:T(4,128)S(1)} %dynamic-slice_bitcast_fusion.9, f32[663,1326]{1,0:T(8,128)S(1)} %or_select_fusion.2, ...), kind=kOutput, calls=%fused_computation.5.clone.1 | convolution fusion | flops 924853184 | bytes 6298408 | tf_op jit(solution)/shard_map/while/body/eval_jaxpr/nij,nlj->nli/dot_general | solution.py:43
  125.2 12.0 %copy.22 = f32[8,4,128,663]{3,2,1,0:T(8,128)} copy(f32[8,4,128,663]{2,3,1,0:T(8,128)} %get-tuple-element.44) | data formatting | bytes 21725184 | tf_op jit(solution)/shard_map/while | solution.py:83
  137.1 16.8 %select_reduce_fusion = f32[32,2,8,663]{3,2,1,0:T(8,128)S(1)} fusion(f32[32,2,8,8,663]{4,3,2,1,0:T(8,128)} %bitcast.31, f32[32,2,8,8]{3,2,1,0:T(8,128)S(1)} %copy.24, pred[32,8]{1,0:T(8,128)(4,1)S(1)} %iota_compare_fusion.2), kind=kLoop, calls=%fused_computation.12 | loop fusion | flops 7807488 | bytes 12237056 | tf_op jit(solution)/shard_map/reduce_max | solution.py:51
  156.7 8.9 %collective-permute-done = f32[64,1326]{1,0:T(8,128)S(1)} collective-permute-done((f32[64,1326]{1,0:T(8,128)S(1)}, f32[64,1326]{1,0:T(8,128)S(1)}, u32[]{:S(2)}, u32[]{:S(2)}) %collective-permute-start) | collective-permute-done | bytes 339488 | tf_op jit(solution)/shard_map/ppermute | solution.py:106
  167.4 8.0 %collective-permute-done.1 = f32[64,1326]{1,0:T(8,128)S(1)} collective-permute-done((f32[64,1326]{1,0:T(8,128)S(1)}, f32[64,1326]{1,0:T(8,128)S(1)}, u32[]{:S(2)}, u32[]{:S(2)}) %collective-permute-start.1) | collective-permute-done | bytes 339488 | tf_op jit(solution)/shard_map/ppermute | solution.py:106
  177.3 7.2 %collective-permute-done.2 = f32[64,1326]{1,0:T(8,128)S(1)} collective-permute-done((f32[64,1326]{1,0:T(8,128)S(1)}, f32[64,1326]{1,0:T(8,128)S(1)}, u32[]{:S(2)}, u32[]{:S(2)}) %collective-permute-start.2) | collective-permute-done | bytes 339488 | tf_op jit(solution)/shard_map/ppermute | solution.py:106
  184.5 2.7 %collective-permute-start.3 = (f32[64,1326]{1,0:T(8,128)S(1)}, f32[64,1326]{1,0:T(8,128)S(1)}, u32[]{:S(2)}, u32[]{:S(2)}) collective-permute-start(f32[64,1326]{1,0:T(8,128)S(1)} %add.29), channel_id=1, source_target_pairs={{0,16},{2,18},{4,20},{6,22},{8,24},{10,26},{12,28},{14,30},{16,0},... | collective-permute-start | bytes 1018376 | tf_op jit(solution)/shard_map/ppermute | solution.py:106
  187.3 13.9 %collective-permute-done.3 = f32[64,1326]{1,0:T(8,128)S(1)} collective-permute-done((f32[64,1326]{1,0:T(8,128)S(1)}, f32[64,1326]{1,0:T(8,128)S(1)}, u32[]{:S(2)}, u32[]{:S(2)}) %collective-permute-start.3) | collective-permute-done | bytes 339488 | tf_op jit(solution)/shard_map/ppermute | solution.py:106
  203.4 3.1 %psum.7 = f32[]{:T(128)} all-reduce(f32[]{:T(128)} %multiply_reduce_fusion), channel_id=1, replica_groups=mesh['node'=16,'hand'=2] {'hand'}, use_global_device_ids=true, to_apply=%region_6.7 | all-reduce | flops 1 | bytes 8 | tf_op jit(solution)/shard_map/psum | solution.py:108
  (78 shorter events, 33.4 us)
Async XLA Ops:
  7.2 28.1 %all-gather.2.cloned.1.call-start = ((), (), s32[]{:S(2)}) async-start(), calls=%async_computation | async-start | bytes 16293888 | tf_op jit(solution)/shard_map/all_gather | solution.py:90
  137.1 17.5 %copy-start.1 = (s32[32]{0:T(128)S(1)}, s32[32]{0:T(128)}, u32[]{:S(2)}) copy-start(s32[32]{0:T(128)} %param.17) | copy-start | bytes 388
  137.1 50.1 %copy-start.2 = (s32[16]{0:T(128)S(1)}, s32[16]{0:T(128)}, u32[]{:S(2)}) copy-start(s32[16]{0:T(128)} %param.18) | copy-start | bytes 196
  137.1 65.0 %copy-start = (f32[16,2,663]{2,1,0:T(2,128)S(1)}, f32[16,2,663]{2,1,0:T(2,128)}, u32[]{:S(2)}) copy-start(f32[16,2,663]{2,1,0:T(2,128)} %param.19) | copy-start | bytes 254596
  154.9 10.7 %collective-permute-start = (f32[64,1326]{1,0:T(8,128)S(1)}, f32[64,1326]{1,0:T(8,128)S(1)}, u32[]{:S(2)}, u32[]{:S(2)}) collective-permute-start(f32[64,1326]{1,0:T(8,128)S(1)} %fusion.5), channel_id=1, source_target_pairs={{0,2},{2,0},{4,6},{6,4},{8,10},{10,8},{12,14},{14,12},{16,18},{18,... | collective-permute-start | bytes 1018376 | tf_op jit(solution)/shard_map/ppermute | solution.py:106
  165.6 9.8 %collective-permute-start.1 = (f32[64,1326]{1,0:T(8,128)S(1)}, f32[64,1326]{1,0:T(8,128)S(1)}, u32[]{:S(2)}, u32[]{:S(2)}) collective-permute-start(f32[64,1326]{1,0:T(8,128)S(1)} %add.27), channel_id=1, source_target_pairs={{0,4},{2,6},{4,0},{6,2},{8,12},{10,14},{12,8},{14,10},{16,20},{18,... | collective-permute-start | bytes 1018376 | tf_op jit(solution)/shard_map/ppermute | solution.py:106
  175.5 9.0 %collective-permute-start.2 = (f32[64,1326]{1,0:T(8,128)S(1)}, f32[64,1326]{1,0:T(8,128)S(1)}, u32[]{:S(2)}, u32[]{:S(2)}) collective-permute-start(f32[64,1326]{1,0:T(8,128)S(1)} %add.28), channel_id=1, source_target_pairs={{0,8},{2,10},{4,12},{6,14},{8,0},{10,2},{12,4},{14,6},{16,24},{18,... | collective-permute-start | bytes 1018376 | tf_op jit(solution)/shard_map/ppermute | solution.py:106
  184.5 16.8 %collective-permute-start.3 = (f32[64,1326]{1,0:T(8,128)S(1)}, f32[64,1326]{1,0:T(8,128)S(1)}, u32[]{:S(2)}, u32[]{:S(2)}) collective-permute-start(f32[64,1326]{1,0:T(8,128)S(1)} %add.29), channel_id=1, source_target_pairs={{0,16},{2,18},{4,20},{6,22},{8,24},{10,26},{12,28},{14,30},{16,0},... | collective-permute-start | bytes 1018376 | tf_op jit(solution)/shard_map/ppermute | solution.py:106
Sparse Core Ops, SparseCore 0:
  9.5 25.7 all-gather.1
